TPU v7x, 128 devices: a whole 4x4x4 slice. The times are simulated.
128 devices in a mesh: seq: 8 (over z_hi, x), batch: 16 (over z_lo, y, core).
Axes of the slice: x: 4, y: 4, z: 4 (z_hi: 2, z_lo: 2; z = z_hi * 2 + z_lo), core: 2. Of those that a mesh axis runs over, the one named last changes fastest.
Arguments:
- attn_out: bfloat16 [65536, 2560], P(('seq', 'batch')), may hold values from -200 to 200
- out_grad: bfloat16 [65536, 2560], P(('seq', 'batch')), may hold values from -6 to 6
- master: float32 [2560, 2560], P(('seq', 'batch')), may hold values from -0.125 to 0.125
- moment_one: float32 [2560, 2560], P(('seq', 'batch')), may hold values from -4 to 4
- moment_two: float32 [2560, 2560], P(('seq', 'batch')), may hold values from 0.002 to 0.05
Outputs:
- input_grad: bfloat16 [65536, 2560], P(('seq', 'batch'))
- new_master: float32 [2560, 2560], P(('seq', 'batch'))
- new_moment_one: float32 [2560, 2560], P(('seq', 'batch'))
- new_moment_two: float32 [2560, 2560], P(('seq', 'batch'))
All inputs are finite; a program needn't handle non-finite values.
Results may differ from a plain program's by a relative error of at most 0.01.
Values may be sent and summed in bfloat16 or wider, within the bound.
A program may use at most 128 MiB of HBM per device.

v0:
```python
import jax
import jax.numpy as jnp
from jax import lax
from jax.sharding import Mesh
from jax.sharding import PartitionSpec as P

DIN = 2560
DOUT = 2560
GRAD_BLOCKS = 4
STEP = 10
BATCH = ("batch_0", "batch_1", "batch_2")
SEQ = ("seq_0", "seq_1")
SEQ_BATCH = ("seq_0", "seq_1", "batch_0", "batch_1", "batch_2")


def laid_out(pieces, dim):
    pieces = jnp.moveaxis(pieces, 0, dim)
    lengths = pieces.shape
    return pieces.reshape(*lengths[:dim], lengths[dim] * lengths[dim + 1], *lengths[dim + 2 :])


def copy_for_each(value, axis):
    devices = lax.axis_size(axis)
    return lax.all_to_all(
        jnp.broadcast_to(value[None], (devices, *value.shape)), axis, 0, 0, tiled=True
    )


def gather_directly(value, axis, dim):
    return laid_out(copy_for_each(value, axis), dim)


def by_axis(value, axes):
    for axis in axes:
        value = lax.psum(value, axis)
    return value


def on_device(attn_out, out_grad, master, moment_one, moment_two):
    shard_weight = master.astype(jnp.bfloat16)
    grouped = gather_directly(shard_weight, BATCH, 0)
    projected = lax.dot_general(
        out_grad,
        lax.all_gather(grouped, SEQ, axis=0, tiled=True),
        (((1,), (1,)), ((), ())),
        preferred_element_type=jnp.float32,
    )
    input_grad = projected.astype(jnp.bfloat16)
    block_width = out_grad.shape[1] // GRAD_BLOCKS
    grad_parts = []
    for block in range(GRAD_BLOCKS):
        grad_cols = out_grad[:, block * block_width : (block + 1) * block_width]
        grad_parts.append(
            lax.psum_scatter(
                lax.dot_general(
                    attn_out,
                    grad_cols,
                    (((0,), (0,)), ((), ())),
                    preferred_element_type=jnp.float32,
                ).astype(jnp.bfloat16),
                SEQ_BATCH,
                scatter_dimension=0,
                tiled=True,
            ).astype(jnp.float32)
        )
    weight_grad = jnp.concatenate(grad_parts, axis=1)
    squares = by_axis(jnp.sum(weight_grad * weight_grad), SEQ_BATCH)
    grad_norm = jnp.sqrt(squares) + 1e-06
    limit = jnp.sqrt(jnp.float32(DIN * DOUT))
    clipped = weight_grad * jnp.minimum(jnp.float32(1.0), limit / grad_norm)
    new_one = 0.9 * moment_one + 0.1 * clipped
    new_two = 0.999 * moment_two + 0.001 * clipped * clipped
    first_hat = new_one / (1.0 - 0.9**STEP)
    second_hat = new_two / (1.0 - 0.999**STEP)
    new_master = master - 0.01 * (first_hat / (jnp.sqrt(second_hat) + 1e-08) + 0.1 * master)
    return (input_grad, new_master, new_one, new_two)


def solution(mesh):
    finer = Mesh(
        mesh.devices.reshape(2, 4, 2, 4, 2), ("seq_0", "seq_1", "batch_0", "batch_1", "batch_2")
    )
    in_specs = (
        P(SEQ_BATCH, None),
        P(SEQ_BATCH, None),
        P(SEQ_BATCH, None),
        P(SEQ_BATCH, None),
        P(SEQ_BATCH, None),
    )
    out_specs = (P(SEQ_BATCH, None), P(SEQ_BATCH, None), P(SEQ_BATCH, None), P(SEQ_BATCH, None))
    return jax.shard_map(
        on_device, mesh=finer, in_specs=in_specs, out_specs=out_specs, check_vma=False
    )
```

profile of v0, /device:TPU:0, one launch (start us, length us, event | category | flops | bytes accessed | tf_op | source)
XLA Modules:
  0.0 438.9 jit_solution(13695303821592365688)
XLA Ops:
  7.2 0.0 copy-start
  7.2 0.0 all-reduce.7.cloned.1.call-start
  7.2 1.7 copy-done
  8.9 0.0 copy-start.4
  8.9 5.1 %convolution_convert_fusion = bf16[2560,640]{1,0:T(8,128)(2,1)} fusion(bf16[512,2560]{1,0:T(8,128)(2,1)S(1)} %copy-done, bf16[512,2560]{1,0:T(8,128)(2,1)} %param.6), kind=kOutput, calls=%fused_computation | convolution fusion | flops 1679360000 | bytes 6553600 | tf_op jit(solution)/shard_map/dot_general | solution.py:55
  14.1 0.0 copy-done.4
  14.1 4.0 convolution_convert_fusion.1
  18.0 4.0 convolution_convert_fusion.2
  22.0 4.0 convolution_convert_fusion.3
  26.0 0.0 copy-start.1
  26.0 0.0 copy-start.3
  26.0 0.0 all-reduce.7.cloned.1.call-update
  26.0 0.0 all-gather.2.cloned.1.call-start
  26.1 173.5 %all-reduce.7.cloned.1.call-done = (bf16[2560,640]{1,0:T(8,128)(2,1)}, bf16[2560,640]{1,0:T(8,128)(2,1)}, bf16[2560,640]{1,0:T(8,128)(2,1)}, bf16[2560,640]{1,0:T(8,128)(2,1)}) async-done(((bf16[2560,640]{1,0:T(8,128)(2,1)}, bf16[2560,640]{1,0:T(8,128)(2,1)}, bf16[2560,640]{1,0:T(8,128)(2,1)}, bf16[2560,640]{1,0:T(8,128)(2,1)}), (bf16[2560,640]{1,0:T(8,128)(2,1)}, bf16[2560,640]{1,0:T(8,128)(2,1)}, ...) | async-done | bytes 13107216
  199.6 0.8 constant_dynamic-slice_fusion.2
  200.5 0.8 constant_dynamic-slice_fusion
  201.3 0.7 fusion.6
  202.0 7.0 %psum.35 = f32[]{:T(128)} all-reduce(f32[]{:T(128)} %fusion.6), channel_id=1, replica_groups=mesh['seq_0'=2,'seq_1'=4,'batch_0'=2,'batch_1'=4,'batch_2'=2] {'seq_0'}, use_global_device_ids=true, to_apply=%region_5.0 | all-reduce | flops 1 | bytes 8 | tf_op jit(solution)/shard_map/psum | solution.py:35
  209.0 10.4 %psum.36 = f32[]{:T(128)} all-reduce(f32[]{:T(128)} %psum.35), channel_id=1, replica_groups=mesh['seq_0'=2,'seq_1'=4,'batch_0'=2,'batch_1'=4,'batch_2'=2] {'seq_1'}, use_global_device_ids=true, to_apply=%region_6.0 | all-reduce | flops 1 | bytes 8 | tf_op jit(solution)/shard_map/psum | solution.py:35
  219.5 5.5 %psum.37 = f32[]{:T(128)} all-reduce(f32[]{:T(128)} %psum.36), channel_id=1, replica_groups=mesh['seq_0'=2,'seq_1'=4,'batch_0'=2,'batch_1'=4,'batch_2'=2] {'batch_0'}, use_global_device_ids=true, to_apply=%region_7.0 | all-reduce | flops 1 | bytes 8 | tf_op jit(solution)/shard_map/psum | solution.py:35
  225.0 10.7 %psum.38 = f32[]{:T(128)} all-reduce(f32[]{:T(128)} %psum.37), channel_id=1, replica_groups=mesh['seq_0'=2,'seq_1'=4,'batch_0'=2,'batch_1'=4,'batch_2'=2] {'batch_1'}, use_global_device_ids=true, to_apply=%region_8.0 | all-reduce | flops 1 | bytes 8 | tf_op jit(solution)/shard_map/psum | solution.py:35
  235.7 3.1 psum.39
  239.5 0.0 copy-done.1
  239.5 0.0 copy-done.2
  239.6 0.0 copy-done.3
  239.6 1.0 multiply_subtract_fusion
  240.5 0.1 broadcast_in_dim.2
  240.7 29.3 %all_to_all.5 = bf16[16,20,2560]{2,1,0:T(8,128)(2,1)} all-to-all(bf16[16,20,2560]{2,1,0:T(8,128)(2,1)S(1)} %broadcast_in_dim.2), channel_id=1, replica_groups=mesh['seq_0'=2,'seq_1'=4,'batch_0'=2,'batch_1'=4,'batch_2'=2] {'batch_0'..., dimensions={0} | all-to-all | bytes 3276800 | tf_op jit(solution)/shard_map/all_to_all | solution.py:24
  270.0 3.5 reshape.12
  273.5 0.0 all-gather.2.cloned.1.call-update
  273.5 146.7 %all-gather.2.cloned.1.call-done = bf16[2560,2560]{1,0:T(8,128)(2,1)} async-done(((bf16[320,2560]{1,0:T(8,128)(2,1)}), bf16[2560,2560]{1,0:T(8,128)(2,1)}) %all-gather.2.cloned.1.call-update) | async-done | bytes 13107216 | tf_op jit(solution)/shard_map/all_gather | solution.py:44
  420.2 11.9 %convolution_convert_fusion.4 = bf16[512,2560]{1,0:T(8,128)(2,1)} fusion(bf16[512,2560]{1,0:T(8,128)(2,1)} %param.6, bf16[2560,2560]{1,0:T(8,128)(2,1)} %all-gather.2.cloned.1.call-done), kind=kOutput, calls=%fused_computation.4 | convolution fusion | flops 6712197120 | bytes 18350080 | tf_op jit(solution)/shard_map/dot_general | solution.py:42
  (1 shorter events, 0.0 us)
Async XLA Ops:
  7.2 1.7 copy-start
  7.2 192.5 %all-reduce.7.cloned.1.call-start = ((), (), s32[]{:S(2)}) async-start(), calls=%async_computation.2 | async-start | bytes 26214400
  8.9 5.2 %copy-start.4 = (bf16[512,2560]{1,0:T(8,128)(2,1)S(1)}, bf16[512,2560]{1,0:T(8,128)(2,1)}, u32[]{:S(2)}) copy-start(bf16[512,2560]{1,0:T(8,128)(2,1)} %param.6) | copy-start | bytes 7864324
  26.0 213.5 %copy-start.1 = (f32[20,2560]{1,0:T(8,128)S(1)}, f32[20,2560]{1,0:T(8,128)}, u32[]{:S(2)}) copy-start(f32[20,2560]{1,0:T(8,128)} %param.7) | copy-start | bytes 614404
  26.0 213.5 %copy-start.2 = (f32[20,2560]{1,0:T(8,128)S(1)}, f32[20,2560]{1,0:T(8,128)}, u32[]{:S(2)}) copy-start(f32[20,2560]{1,0:T(8,128)} %param.8) | copy-start | bytes 614404
  26.0 213.5 %copy-start.3 = (f32[20,2560]{1,0:T(8,128)S(1)}, f32[20,2560]{1,0:T(8,128)}, u32[]{:S(2)}) copy-start(f32[20,2560]{1,0:T(8,128)} %param.9) | copy-start | bytes 614404
  26.0 394.1 %all-gather.2.cloned.1.call-start = ((), (), s32[]{:S(2)}) async-start(), calls=%async_computation.1 | async-start | bytes 14745600 | tf_op jit(solution)/shard_map/all_gather | solution.py:44
Sparse Core Ops, SparseCore 0:
  26.2 173.4 all-reduce.6
  273.7 146.4 all-gather.1
where the time goes:
time: 439 us
  waiting for transfers between devices  320 us (73%)
  blocking collectives  66.2 us (15%)
  matrix products  29 us (7%)
  between operations  14.8 us (3%)
  local copies, waits for them, and re-layouts  6.99 us (2%)
    unnamed x3, waiting for transfers between devices  174 us
    all_gather x1, waiting for transfers between devices, on_device(): lax.all_gather(grouped, SEQ, axis=0, tiled=True)  147 us
    psum x5, blocking collectives, by_axis(): value = lax.psum(value, axis)  36.8 us
    all_to_all x1, blocking collectives, copy_for_each(): lax.all_to_all(jnp.broadcast_to(value[None], (devices, *value.shape)), ax...  29.3 us
    dot_general x4, matrix products, on_device(): lax.dot_general(attn_out, grad_cols, (((0,), (0,)), ((), ())), preferred_...  17.1 us
    dot_general x1, matrix products, on_device(): lax.dot_general(out_grad, lax.all_gather(grouped, SEQ, axis=0, tiled=True...  11.9 us
  transfers between devices with their start and end apart: 2, of which 2 were waited for; matrix products, arithmetic and copies ran while one was open for 0% of the time, Pallas kernels for 0%

commit v1 on v0

--- a/solution.py
+++ b/solution.py
@@ -11,6 +11,12 @@
 BATCH = ("batch_0", "batch_1", "batch_2")
 SEQ = ("seq_0", "seq_1")
 SEQ_BATCH = ("seq_0", "seq_1", "batch_0", "batch_1", "batch_2")
+
+
+def summed_here(x, mesh_axis):
+    parts = lax.all_gather(x, mesh_axis, axis=0, tiled=False)
+    summed = parts.sum(axis=0)
+    return summed
 
 
 def laid_out(pieces, dim):
@@ -32,7 +38,7 @@
 
 def by_axis(value, axes):
     for axis in axes:
-        value = lax.psum(value, axis)
+        value = summed_here(value, axis)
     return value
 
 

time: 439 us -> 449 us (1.023)
  local copies, waits for them, and re-layouts: 6.99 us -> 17.5 us
    psum x5 -> x0, blocking collectives: 36.8 us -> none  [by_axis(): value = lax.psum(value, axis)]
    unnamed x0 -> x5, blocking collectives: none -> 33.7 us
    unnamed x12 -> x37, local copies, waits for them, and re-layouts: 3.35 us -> 13.8 us
where the time goes in v1:
time: 449 us; the launch traced here: 448 us
  waiting for transfers between devices  319 us (71%)
  blocking collectives  63 us (14%)
  matrix products  29 us (6%)
  local copies, waits for them, and re-layouts  17.5 us (4%)
  between operations  14.9 us (3%)
  other arithmetic  4.67 us (1%)
    unnamed x3, waiting for transfers between devices  172 us
    all_gather x1, waiting for transfers between devices, on_device(): lax.all_gather(grouped, SEQ, axis=0, tiled=True)  147 us
    unnamed x5, blocking collectives  33.7 us
    all_to_all x1, blocking collectives, copy_for_each(): lax.all_to_all(jnp.broadcast_to(value[None], (devices, *value.shape)), ax...  29.3 us
    dot_general x4, matrix products, on_device(): lax.dot_general(attn_out, grad_cols, (((0,), (0,)), ((), ())), preferred_...  17.1 us
    unnamed x37, local copies, waits for them, and re-layouts  13.8 us
    dot_general x1, matrix products, on_device(): lax.dot_general(out_grad, lax.all_gather(grouped, SEQ, axis=0, tiled=True...  11.9 us
  transfers between devices with their start and end apart: 2, of which 2 were waited for; matrix products, arithmetic and copies ran while one was open for 0% of the time, Pallas kernels for 0%

profile of v1, /device:TPU:0, one launch (start us, length us, event | category | flops | bytes accessed | tf_op | source)
XLA Modules:
  0.0 448.2 jit_solution(2176065000952740465)
XLA Ops:
  7.2 1.7 copy-done
  8.9 5.1 %convolution_convert_fusion = bf16[2560,640]{1,0:T(8,128)(2,1)} fusion(bf16[512,2560]{1,0:T(8,128)(2,1)S(1)} %copy-done, bf16[512,2560]{1,0:T(8,128)(2,1)} %param.6), kind=kOutput, calls=%fused_computation | convolution fusion | flops 1679360000 | bytes 6553600 | tf_op jit(solution)/shard_map/dot_general | solution.py:61
  14.1 4.0 convolution_convert_fusion.1
  18.0 4.0 convolution_convert_fusion.2
  22.0 4.0 convolution_convert_fusion.3
  27.3 172.4 %all-reduce.12.cloned.1.call-done = (bf16[2560,640]{1,0:T(8,128)(2,1)}, bf16[2560,640]{1,0:T(8,128)(2,1)}, bf16[2560,640]{1,0:T(8,128)(2,1)}, bf16[2560,640]{1,0:T(8,128)(2,1)}) async-done(((bf16[2560,640]{1,0:T(8,128)(2,1)}, bf16[2560,640]{1,0:T(8,128)(2,1)}, bf16[2560,640]{1,0:T(8,128)(2,1)}, bf16[2560,640]{1,0:T(8,128)(2,1)}), (bf16[2560,640]{1,0:T(8,128)(2,1)}, bf16[2560,640]{1,0:T(8,128)(2,1)}, ...) | async-done | bytes 13107216
  199.7 0.8 constant_dynamic-slice_fusion.2
  200.5 0.8 constant_dynamic-slice_fusion
  201.4 0.7 fusion.6
  202.0 1.4 dynamic-update-slice
  203.4 0.6 dynamic-slice.1
  204.0 6.4 %all-reduce = f32[2]{0:T(128)S(1)} all-reduce(f32[2]{0:T(128)S(1)} %dynamic-update-slice), channel_id=1, replica_groups=mesh['seq_0'=2,'seq_1'=4,'batch_0'=2,'batch_1'=4,'batch_2'=2] {'seq_0'}, use_global_device_ids=true, to_apply=%add | all-reduce | flops 2 | bytes 16
  210.4 0.6 reduce_sum.55
  211.0 1.4 dynamic-update-slice.1
  212.4 0.6 dynamic-slice.2
  213.0 9.8 %all-reduce.1 = f32[4]{0:T(128)S(1)} all-reduce(f32[4]{0:T(128)S(1)} %dynamic-update-slice.1), channel_id=1, replica_groups=mesh['seq_0'=2,'seq_1'=4,'batch_0'=2,'batch_1'=4,'batch_2'=2] {'seq_1'}, use_global_device_ids=true, to_apply=%add.1 | all-reduce | flops 4 | bytes 32
  222.8 0.6 reduce_sum.56
  223.4 1.4 dynamic-update-slice.2
  224.8 0.6 dynamic-slice.3
  225.4 4.9 %all-reduce.2 = f32[2]{0:T(128)S(1)} all-reduce(f32[2]{0:T(128)S(1)} %dynamic-update-slice.2), channel_id=1, replica_groups=mesh['seq_0'=2,'seq_1'=4,'batch_0'=2,'batch_1'=4,'batch_2'=2] {'batch_0'}, use_global_device_ids=true, to_apply=%add.2 | all-reduce | flops 2 | bytes 16
  230.3 0.6 reduce_sum.57
  230.9 1.4 dynamic-update-slice.3
  232.9 10.1 %all-reduce.3 = f32[4]{0:T(128)S(1)} all-reduce(f32[4]{0:T(128)S(1)} %dynamic-update-slice.3), channel_id=1, replica_groups=mesh['seq_0'=2,'seq_1'=4,'batch_0'=2,'batch_1'=4,'batch_2'=2] {'batch_1'}, use_global_device_ids=true, to_apply=%add.3 | all-reduce | flops 4 | bytes 32
  243.0 0.6 reduce_sum.58
  243.6 1.4 dynamic-update-slice.4
  245.0 2.4 all-reduce.4
  247.5 0.6 reduce_sum.59
  248.8 1.0 multiply_subtract_fusion
  249.9 29.3 %all_to_all.5 = bf16[16,20,2560]{2,1,0:T(8,128)(2,1)} all-to-all(bf16[16,20,2560]{2,1,0:T(8,128)(2,1)S(1)} %broadcast_in_dim.2), channel_id=1, replica_groups=mesh['seq_0'=2,'seq_1'=4,'batch_0'=2,'batch_1'=4,'batch_2'=2] {'batch_0'..., dimensions={0} | all-to-all | bytes 3276800 | tf_op jit(solution)/shard_map/all_to_all | solution.py:30
  279.3 3.5 reshape.12
  282.8 146.7 %all-gather.2.cloned.1.call-done = bf16[2560,2560]{1,0:T(8,128)(2,1)} async-done(((bf16[320,2560]{1,0:T(8,128)(2,1)}), bf16[2560,2560]{1,0:T(8,128)(2,1)}) %all-gather.2.cloned.1.call-update) | async-done | bytes 13107216 | tf_op jit(solution)/shard_map/all_gather | solution.py:50
  429.5 11.9 %convolution_convert_fusion.4 = bf16[512,2560]{1,0:T(8,128)(2,1)} fusion(bf16[512,2560]{1,0:T(8,128)(2,1)} %param.6, bf16[2560,2560]{1,0:T(8,128)(2,1)} %all-gather.2.cloned.1.call-done), kind=kOutput, calls=%fused_computation.4 | convolution fusion | flops 6712197120 | bytes 18350080 | tf_op jit(solution)/shard_map/dot_general | solution.py:48
  (31 shorter events, 2.0 us)
Async XLA Ops:
  7.2 1.7 copy-start
  7.2 192.5 %all-reduce.12.cloned.1.call-start = ((), (), s32[]{:S(2)}) async-start(), calls=%async_computation.2 | async-start | bytes 26214400
  8.9 5.2 %copy-start.4 = (bf16[512,2560]{1,0:T(8,128)(2,1)S(1)}, bf16[512,2560]{1,0:T(8,128)(2,1)}, u32[]{:S(2)}) copy-start(bf16[512,2560]{1,0:T(8,128)(2,1)} %param.6) | copy-start | bytes 7864324
  26.0 0.7 copy-start.9
  26.0 177.4 %copy-start.8 = (u32[128]{0:T(128)S(1)}, u32[128]{0:T(128)}, u32[]{:S(2)}) copy-start(u32[128]{0:T(128)} %constant.36) | copy-start | bytes 1540
  26.0 186.4 %copy-start.7 = (u32[128]{0:T(128)S(1)}, u32[128]{0:T(128)}, u32[]{:S(2)}) copy-start(u32[128]{0:T(128)} %constant.41) | copy-start | bytes 1540
  26.0 198.8 %copy-start.6 = (u32[128]{0:T(128)S(1)}, u32[128]{0:T(128)}, u32[]{:S(2)}) copy-start(u32[128]{0:T(128)} %constant.46) | copy-start | bytes 1540
  26.0 206.3 %copy-start.5 = (u32[128]{0:T(128)S(1)}, u32[128]{0:T(128)}, u32[]{:S(2)}) copy-start(u32[128]{0:T(128)} %constant.51) | copy-start | bytes 1540
  26.0 222.8 %copy-start.1 = (f32[20,2560]{1,0:T(8,128)S(1)}, f32[20,2560]{1,0:T(8,128)}, u32[]{:S(2)}) copy-start(f32[20,2560]{1,0:T(8,128)} %param.7) | copy-start | bytes 614404
  26.1 222.8 %copy-start.2 = (f32[20,2560]{1,0:T(8,128)S(1)}, f32[20,2560]{1,0:T(8,128)}, u32[]{:S(2)}) copy-start(f32[20,2560]{1,0:T(8,128)} %param.8) | copy-start | bytes 614404
  26.1 222.7 %copy-start.3 = (f32[20,2560]{1,0:T(8,128)S(1)}, f32[20,2560]{1,0:T(8,128)}, u32[]{:S(2)}) copy-start(f32[20,2560]{1,0:T(8,128)} %param.9) | copy-start | bytes 614404
  26.1 403.4 %all-gather.2.cloned.1.call-start = ((), (), s32[]{:S(2)}) async-start(), calls=%async_computation.1 | async-start | bytes 14745600 | tf_op jit(solution)/shard_map/all_gather | solution.py:50
Sparse Core Ops, SparseCore 0:
  26.2 173.4 all-reduce.11
  282.9 146.4 all-gather.1
